TPU v7x, 128 devices: a whole 4x4x4 slice. The times are simulated.
128 devices in a mesh: dp: 1, sp: 128 (over z, y, x, core).
Axes of the slice: x: 4, y: 4, z: 4, core: 2. Of those that a mesh axis runs over, the one named last changes fastest.
Arguments:
- signal: bfloat16 [131072, 1024], P(('dp', 'sp'))
- w_first: bfloat16 [11, 2048, 2, 64, 64], P(None, 'sp')
- w_second: bfloat16 [11, 2048, 2, 64, 64], P(None, 'sp')
Outputs:
- output: bfloat16 [131072, 1024], P(('dp', 'sp'))
All inputs are finite; a program needn't handle non-finite values.
Results may differ from a plain program's by a relative error of at most 0.02.
Values are sent between devices in bfloat16 or wider.
A program may use at most 1 GiB of HBM per device.

v0:
```python
import jax
import jax.numpy as jnp
from jax import lax
from jax.sharding import PartitionSpec as P


def local_partner(act_blocks, distance):
    num_blocks = act_blocks.shape[0]
    grouped = act_blocks.reshape(num_blocks // (2 * distance), 2, distance, act_blocks.shape[1], act_blocks.shape[2])
    return grouped[:, ::-1].reshape(act_blocks.shape)


def mix_blocks(act_blocks, partner, weights):
    own_part = jnp.einsum("lij,ljc->lic", weights[:, 0], act_blocks, preferred_element_type=jnp.float32)
    cross_part = jnp.einsum("lij,ljc->lic", weights[:, 1], partner, preferred_element_type=jnp.float32)
    return (own_part + cross_part).astype(jnp.bfloat16)


def solution(mesh):
    groups = mesh.shape["sp"]

    def apply_map(act_blocks, weights, distances):
        local_blocks = act_blocks.shape[0]
        for stage, distance in enumerate(distances):
            if distance < local_blocks:
                partner = local_partner(act_blocks, distance)
            else:
                dev_step = distance // local_blocks
                pairing = [(device, device ^ dev_step) for device in range(groups)]
                partner = lax.ppermute(act_blocks, "sp", pairing)
            act_blocks = mix_blocks(act_blocks, partner, weights[stage])
        return act_blocks

    def device_program(signal, w_first, w_second):
        stages = w_first.shape[0]
        local_blocks = w_first.shape[1]
        block_rows = w_first.shape[3]
        act_blocks = signal.reshape(local_blocks, block_rows, signal.shape[1])
        dist_down = [2 ** (stages - 1 - level) for level in range(stages)]
        hidden = apply_map(act_blocks, w_first, dist_down)
        hidden = jax.nn.gelu(hidden.astype(jnp.float32), approximate=False).astype(jnp.bfloat16)
        result = apply_map(hidden, w_second, dist_down[::-1])
        return result.reshape(signal.shape)

    row_spec = P(("dp", "sp"), None)
    weight_spec = P(None, "sp", None, None, None)
    return jax.shard_map(device_program, mesh=mesh, in_specs=(row_spec, weight_spec, weight_spec), out_specs=row_spec, check_vma=False)
```

profile of v0, /device:TPU:1, one launch (start us, length us, event | category | flops | bytes accessed | tf_op | source)
XLA Modules:
  0.0 623.0 jit_solution(3803391946133367949)
XLA Ops:
  0.0 4.4 collective-permute-start
  4.4 4.0 fusion.56
  9.2 40.6 %collective-permute-done = bf16[16,64,1024]{2,1,0:T(8,128)(2,1)S(1)} collective-permute-done((bf16[16,64,1024]{2,1,0:T(8,128)(2,1)}, bf16[16,64,1024]{2,1,0:T(8,128)(2,1)S(1)}, u32[]{:S(2)}, u32[]{:S(2)}) %collective-permute-start) | collective-permute-done | bytes 2097184 | tf_op jit(solution)/shard_map/ppermute | solution.py:30
  52.1 44.2 %collective-permute-done.1 = bf16[16,64,1024]{2,1,0:T(8,128)(2,1)S(1)} collective-permute-done((bf16[16,64,1024]{2,1,0:T(8,128)(2,1)S(1)}, bf16[16,64,1024]{2,1,0:T(8,128)(2,1)S(1)}, u32[]{:S(2)}, u32[]{:S(2)}) %collective-permute-start.1) | collective-permute-done | bytes 2097184 | tf_op jit(solution)/shard_map/ppermute | solution.py:30
  97.0 3.0 collective-permute-start.2
  100.7 42.7 %collective-permute-done.2 = bf16[16,64,1024]{2,1,0:T(8,128)(2,1)S(1)} collective-permute-done((bf16[16,64,1024]{2,1,0:T(8,128)(2,1)S(1)}, bf16[16,64,1024]{2,1,0:T(8,128)(2,1)S(1)}, u32[]{:S(2)}, u32[]{:S(2)}) %collective-permute-start.2) | collective-permute-done | bytes 2097184 | tf_op jit(solution)/shard_map/ppermute | solution.py:30
  144.2 1.4 collective-permute-start.3
  146.3 41.7 %collective-permute-done.3 = bf16[16,64,1024]{2,1,0:T(8,128)(2,1)S(1)} collective-permute-done((bf16[16,64,1024]{2,1,0:T(8,128)(2,1)S(1)}, bf16[16,64,1024]{2,1,0:T(8,128)(2,1)S(1)}, u32[]{:S(2)}, u32[]{:S(2)}) %collective-permute-start.3) | collective-permute-done | bytes 2097184 | tf_op jit(solution)/shard_map/ppermute | solution.py:30
  188.7 2.8 collective-permute-start.4
  192.3 40.9 %collective-permute-done.4 = bf16[16,64,1024]{2,1,0:T(8,128)(2,1)S(1)} collective-permute-done((bf16[16,64,1024]{2,1,0:T(8,128)(2,1)S(1)}, bf16[16,64,1024]{2,1,0:T(8,128)(2,1)S(1)}, u32[]{:S(2)}, u32[]{:S(2)}) %collective-permute-start.4) | collective-permute-done | bytes 2097184 | tf_op jit(solution)/shard_map/ppermute | solution.py:30
  233.9 1.3 collective-permute-start.5
  235.9 42.4 %collective-permute-done.5 = bf16[16,64,1024]{2,1,0:T(8,128)(2,1)S(1)} collective-permute-done((bf16[16,64,1024]{2,1,0:T(8,128)(2,1)S(1)}, bf16[16,64,1024]{2,1,0:T(8,128)(2,1)S(1)}, u32[]{:S(2)}, u32[]{:S(2)}) %collective-permute-start.5) | collective-permute-done | bytes 2097184 | tf_op jit(solution)/shard_map/ppermute | solution.py:30
  279.1 5.5 collective-permute-start.6
  284.5 0.9 copy.78
  286.3 1.0 copy_bitcast_fusion.8
  287.3 2.7 fusion.55
  290.0 1.1 copy_bitcast_fusion.11
  291.1 1.1 copy_bitcast_fusion.13
  293.6 1.6 rev.24
  295.2 1.8 fusion.40
  297.7 1.6 rev.25
  299.3 1.8 fusion.41
  301.8 1.6 rev.26
  303.4 1.8 fusion.42
  305.9 1.6 rev.27
  307.5 1.8 fusion.43
  309.3 9.9 %fusion.2 = bf16[16,64,1024]{2,1,0:T(8,128)(2,1)S(1)} fusion(f32[16,1024,64]{1,2,0:T(8,128)S(1)} %fusion.43, bf16[16,64,1024]{2,1,0:T(8,128)(2,1)S(1)} %bitcast.437, bf16[16,2,64,64]{3,2,0,1:T(8,128)(2,1)S(1)} %bitcast.439), kind=kOutput, calls=%fused_computation.5 | convolution fusion | flops 205520896 | bytes 8650752 | tf_op jit(solution)/shard_map/lij,ljc->lic/dot_general | solution.py:15
  319.2 1.6 rev.28
  320.8 1.8 fusion.44
  323.3 1.6 rev.29
  324.9 1.8 fusion.45
  327.4 1.6 rev.30
  329.0 1.8 fusion.46
  331.5 1.6 rev.31
  333.1 1.8 fusion.47
  336.7 3.2 collective-permute-done.7
  340.6 1.3 collective-permute-start.8
  342.6 45.2 %collective-permute-done.8 = bf16[16,64,1024]{2,1,0:T(8,128)(2,1)S(1)} collective-permute-done((bf16[16,64,1024]{2,1,0:T(8,128)(2,1)S(1)}, bf16[16,64,1024]{2,1,0:T(8,128)(2,1)S(1)}, u32[]{:S(2)}, u32[]{:S(2)}) %collective-permute-start.8) | collective-permute-done | bytes 2097184 | tf_op jit(solution)/shard_map/ppermute | solution.py:30
  388.4 2.1 collective-permute-start.9
  391.2 45.2 %collective-permute-done.9 = bf16[16,64,1024]{2,1,0:T(8,128)(2,1)S(1)} collective-permute-done((bf16[16,64,1024]{2,1,0:T(8,128)(2,1)S(1)}, bf16[16,64,1024]{2,1,0:T(8,128)(2,1)S(1)}, u32[]{:S(2)}, u32[]{:S(2)}) %collective-permute-start.9) | collective-permute-done | bytes 2097184 | tf_op jit(solution)/shard_map/ppermute | solution.py:30
  437.2 1.4 collective-permute-start.10
  439.3 43.1 %collective-permute-done.10 = bf16[16,64,1024]{2,1,0:T(8,128)(2,1)S(1)} collective-permute-done((bf16[16,64,1024]{2,1,0:T(8,128)(2,1)S(1)}, bf16[16,64,1024]{2,1,0:T(8,128)(2,1)S(1)}, u32[]{:S(2)}, u32[]{:S(2)}) %collective-permute-start.10) | collective-permute-done | bytes 2097184 | tf_op jit(solution)/shard_map/ppermute | solution.py:30
  483.0 3.0 collective-permute-start.11
  486.8 42.1 %collective-permute-done.11 = bf16[16,64,1024]{2,1,0:T(8,128)(2,1)S(1)} collective-permute-done((bf16[16,64,1024]{2,1,0:T(8,128)(2,1)S(1)}, bf16[16,64,1024]{2,1,0:T(8,128)(2,1)S(1)}, u32[]{:S(2)}, u32[]{:S(2)}) %collective-permute-start.11) | collective-permute-done | bytes 2097184 | tf_op jit(solution)/shard_map/ppermute | solution.py:30
  530.6 42.2 %collective-permute-done.12 = bf16[16,64,1024]{2,1,0:T(8,128)(2,1)S(1)} collective-permute-done((bf16[16,64,1024]{2,1,0:T(8,128)(2,1)S(1)}, bf16[16,64,1024]{2,1,0:T(8,128)(2,1)S(1)}, u32[]{:S(2)}, u32[]{:S(2)}) %collective-permute-start.12) | collective-permute-done | bytes 2097184 | tf_op jit(solution)/shard_map/ppermute | solution.py:30
  573.5 2.3 collective-permute-start.13
  576.5 44.0 %collective-permute-done.13 = bf16[16,64,1024]{2,1,0:T(8,128)(2,1)S(1)} collective-permute-done((bf16[16,64,1024]{2,1,0:T(8,128)(2,1)S(1)}, bf16[16,64,1024]{2,1,0:T(8,128)(2,1)S(1)}, u32[]{:S(2)}, u32[]{:S(2)}) %collective-permute-start.13) | collective-permute-done | bytes 2097184 | tf_op jit(solution)/shard_map/ppermute | solution.py:30
  620.6 2.0 add_convert_fusion
  (102 shorter events, 26.4 us)
Async XLA Ops:
  0.0 8.5 %copy-start.7 = (bf16[1024,1024]{1,0:T(8,128)(2,1)S(1)}, bf16[1024,1024]{1,0:T(8,128)(2,1)}, u32[]{:S(2)}) copy-start(bf16[1024,1024]{1,0:T(8,128)(2,1)} %param.3) | copy-start | bytes 6291460
  0.0 49.8 %collective-permute-start = (bf16[16,64,1024]{2,1,0:T(8,128)(2,1)}, bf16[16,64,1024]{2,1,0:T(8,128)(2,1)S(1)}, u32[]{:S(2)}, u32[]{:S(2)}) collective-permute-start(bf16[16,64,1024]{2,1,0:T(8,128)(2,1)} %bitcast.405), channel_id=1, source_target_pairs={{0,64},{1,65},{2,66},{3,67},{4,68},{5,69},{6,70},{7,71},{8,72},{9,... | collective-permute-start | bytes 6291464 | tf_op jit(solution)/shard_map/ppermute | solution.py:30
  50.5 45.8 %collective-permute-start.1 = (bf16[16,64,1024]{2,1,0:T(8,128)(2,1)S(1)}, bf16[16,64,1024]{2,1,0:T(8,128)(2,1)S(1)}, u32[]{:S(2)}, u32[]{:S(2)}) collective-permute-start(bf16[16,64,1024]{2,1,0:T(8,128)(2,1)S(1)} %add_convert_fusion.21), channel_id=1, source_target_pairs={{0,32},{1,33},{2,34},{3,35},{4,36},{5,37},{6,38},{7,39},{8,40},{9,... | collective-permute-start | bytes 6291464 | tf_op jit(solution)/shard_map/ppermute | solution.py:30
  97.0 46.4 %collective-permute-start.2 = (bf16[16,64,1024]{2,1,0:T(8,128)(2,1)S(1)}, bf16[16,64,1024]{2,1,0:T(8,128)(2,1)S(1)}, u32[]{:S(2)}, u32[]{:S(2)}) collective-permute-start(bf16[16,64,1024]{2,1,0:T(8,128)(2,1)S(1)} %bitcast.386), channel_id=1, source_target_pairs={{0,16},{1,17},{2,18},{3,19},{4,20},{5,21},{6,22},{7,23},{8,24},{9,... | collective-permute-start | bytes 6291464 | tf_op jit(solution)/shard_map/ppermute | solution.py:30
  144.2 43.8 %collective-permute-start.3 = (bf16[16,64,1024]{2,1,0:T(8,128)(2,1)S(1)}, bf16[16,64,1024]{2,1,0:T(8,128)(2,1)S(1)}, u32[]{:S(2)}, u32[]{:S(2)}) collective-permute-start(bf16[16,64,1024]{2,1,0:T(8,128)(2,1)S(1)} %bitcast.387), channel_id=1, source_target_pairs={{0,8},{1,9},{2,10},{3,11},{4,12},{5,13},{6,14},{7,15},{8,0},{9,1},... | collective-permute-start | bytes 6291464 | tf_op jit(solution)/shard_map/ppermute | solution.py:30
  188.7 44.5 %collective-permute-start.4 = (bf16[16,64,1024]{2,1,0:T(8,128)(2,1)S(1)}, bf16[16,64,1024]{2,1,0:T(8,128)(2,1)S(1)}, u32[]{:S(2)}, u32[]{:S(2)}) collective-permute-start(bf16[16,64,1024]{2,1,0:T(8,128)(2,1)S(1)} %bitcast.388), channel_id=1, source_target_pairs={{0,4},{1,5},{2,6},{3,7},{4,0},{5,1},{6,2},{7,3},{8,12},{9,13},{10,... | collective-permute-start | bytes 6291464 | tf_op jit(solution)/shard_map/ppermute | solution.py:30
  233.9 44.5 %collective-permute-start.5 = (bf16[16,64,1024]{2,1,0:T(8,128)(2,1)S(1)}, bf16[16,64,1024]{2,1,0:T(8,128)(2,1)S(1)}, u32[]{:S(2)}, u32[]{:S(2)}) collective-permute-start(bf16[16,64,1024]{2,1,0:T(8,128)(2,1)S(1)} %bitcast.389), channel_id=1, source_target_pairs={{0,2},{1,3},{2,0},{3,1},{4,6},{5,7},{6,4},{7,5},{8,10},{9,11},{10,... | collective-permute-start | bytes 6291464 | tf_op jit(solution)/shard_map/ppermute | solution.py:30
  235.2 52.1 %slice-start = ((s8[5767168]{0:T(1024)(128)(4,1)}), s8[4194304]{0:T(1024)(128)(4,1)S(1)}, s32[]{:S(2)}) async-start(s8[5767168]{0:T(1024)(128)(4,1)} %bitcast.403), calls=%async_computation | async-start | bytes 8388608
  235.9 51.4 %slice-start.1 = ((s8[5767168]{0:T(1024)(128)(4,1)}), s8[1572864]{0:T(1024)(128)(4,1)S(1)}, s32[]{:S(2)}) async-start(s8[5767168]{0:T(1024)(128)(4,1)} %bitcast.403), calls=%async_computation.1 | async-start | bytes 3145728
  279.1 13.8 %collective-permute-start.6 = (bf16[16,64,1024]{2,1,0:T(8,128)(2,1)S(1)}, bf16[16,64,1024]{2,1,0:T(8,128)(2,1)S(1)}, u32[]{:S(2)}, u32[]{:S(2)}) collective-permute-start(bf16[16,64,1024]{2,1,0:T(8,128)(2,1)S(1)} %bitcast.384), channel_id=1, source_target_pairs={{0,1},{1,0},{2,3},{3,2},{4,5},{5,4},{6,7},{7,6},{8,9},{9,8},{10,11... | collective-permute-start | bytes 6291464 | tf_op jit(solution)/shard_map/ppermute | solution.py:30
  295.2 1.8 copy-start.3
  295.2 1.8 copy-start.13
  299.3 1.8 copy-start.4
  299.3 1.8 copy-start.20
  303.4 1.8 copy-start
  303.4 1.8 copy-start.18
  307.5 1.8 copy-start.14
  307.5 1.8 copy-start.21
  320.8 1.8 copy-start.5
  320.8 1.8 copy-start.19
  324.9 1.8 copy-start.1
  324.9 1.8 copy-start.17
  329.0 1.8 copy-start.6
  329.0 1.8 copy-start.16
  333.1 1.8 copy-start.2
  333.1 1.8 copy-start.15
  334.9 1.0 copy-start.12
  335.6 4.2 collective-permute-start.7
  339.9 2.0 copy-start.11
  340.6 47.1 %collective-permute-start.8 = (bf16[16,64,1024]{2,1,0:T(8,128)(2,1)S(1)}, bf16[16,64,1024]{2,1,0:T(8,128)(2,1)S(1)}, u32[]{:S(2)}, u32[]{:S(2)}) collective-permute-start(bf16[16,64,1024]{2,1,0:T(8,128)(2,1)S(1)} %bitcast.391), channel_id=1, source_target_pairs={{0,2},{1,3},{2,0},{3,1},{4,6},{5,7},{6,4},{7,5},{8,10},{9,11},{10,... | collective-permute-start | bytes 6291464 | tf_op jit(solution)/shard_map/ppermute | solution.py:30
  387.7 2.8 copy-start.10
  388.4 48.0 %collective-permute-start.9 = (bf16[16,64,1024]{2,1,0:T(8,128)(2,1)S(1)}, bf16[16,64,1024]{2,1,0:T(8,128)(2,1)S(1)}, u32[]{:S(2)}, u32[]{:S(2)}) collective-permute-start(bf16[16,64,1024]{2,1,0:T(8,128)(2,1)S(1)} %bitcast.392), channel_id=1, source_target_pairs={{0,4},{1,5},{2,6},{3,7},{4,0},{5,1},{6,2},{7,3},{8,12},{9,13},{10,... | collective-permute-start | bytes 6291464 | tf_op jit(solution)/shard_map/ppermute | solution.py:30
  436.5 2.1 copy-start.9
  437.2 45.2 %collective-permute-start.10 = (bf16[16,64,1024]{2,1,0:T(8,128)(2,1)S(1)}, bf16[16,64,1024]{2,1,0:T(8,128)(2,1)S(1)}, u32[]{:S(2)}, u32[]{:S(2)}) collective-permute-start(bf16[16,64,1024]{2,1,0:T(8,128)(2,1)S(1)} %bitcast.393), channel_id=1, source_target_pairs={{0,8},{1,9},{2,10},{3,11},{4,12},{5,13},{6,14},{7,15},{8,0},{9,1},... | collective-permute-start | bytes 6291464 | tf_op jit(solution)/shard_map/ppermute | solution.py:30
  482.3 3.7 copy-start.8
  483.0 45.8 %collective-permute-start.11 = (bf16[16,64,1024]{2,1,0:T(8,128)(2,1)S(1)}, bf16[16,64,1024]{2,1,0:T(8,128)(2,1)S(1)}, u32[]{:S(2)}, u32[]{:S(2)}) collective-permute-start(bf16[16,64,1024]{2,1,0:T(8,128)(2,1)S(1)} %bitcast.394), channel_id=1, source_target_pairs={{0,16},{1,17},{2,18},{3,19},{4,20},{5,21},{6,22},{7,23},{8,24},{9,... | collective-permute-start | bytes 6291464 | tf_op jit(solution)/shard_map/ppermute | solution.py:30
  529.6 43.2 %collective-permute-start.12 = (bf16[16,64,1024]{2,1,0:T(8,128)(2,1)S(1)}, bf16[16,64,1024]{2,1,0:T(8,128)(2,1)S(1)}, u32[]{:S(2)}, u32[]{:S(2)}) collective-permute-start(bf16[16,64,1024]{2,1,0:T(8,128)(2,1)S(1)} %bitcast.395), channel_id=1, source_target_pairs={{0,32},{1,33},{2,34},{3,35},{4,36},{5,37},{6,38},{7,39},{8,40},{9,... | collective-permute-start | bytes 6291464 | tf_op jit(solution)/shard_map/ppermute | solution.py:30
  573.5 47.1 %collective-permute-start.13 = (bf16[16,64,1024]{2,1,0:T(8,128)(2,1)S(1)}, bf16[16,64,1024]{2,1,0:T(8,128)(2,1)S(1)}, u32[]{:S(2)}, u32[]{:S(2)}) collective-permute-start(bf16[16,64,1024]{2,1,0:T(8,128)(2,1)S(1)} %bitcast.385), channel_id=1, source_target_pairs={{0,64},{1,65},{2,66},{3,67},{4,68},{5,69},{6,70},{7,71},{8,72},{9,... | collective-permute-start | bytes 6291464 | tf_op jit(solution)/shard_map/ppermute | solution.py:30
where the time goes:
time: 635 us; the launch traced here: 623 us
  waiting for transfers between devices  518 us (82%)
  matrix products  49.7 us (8%)
  starting transfers between devices  29.6 us (5%)
  local copies, waits for them, and re-layouts  25.1 us (4%)
    ppermute x14, waiting for transfers between devices, apply_map(): partner = lax.ppermute(act_blocks, 'sp', pairing)  518 us
    ppermute x14, starting transfers between devices, apply_map(): partner = lax.ppermute(act_blocks, 'sp', pairing)  29.6 us
    dot_general x22, matrix products, mix_blocks(): jnp.einsum('lij,ljc->lic', weights[:, 1], partner, preferred_element_type...  25.8 us
    dot_general x22, matrix products, mix_blocks(): jnp.einsum('lij,ljc->lic', weights[:, 0], act_blocks, preferred_element_t...  23.9 us
    rev x8, local copies, waits for them, and re-layouts, local_partner(): return grouped[:, ::-1].reshape(act_blocks.shape)  12.7 us
  transfers between devices with their start and end apart: 14, of which 13 were waited for; matrix products, arithmetic and copies ran while one was open for 3% of the time, Pallas kernels for 0%

commit v1 on v0

v1 whole, which is shorter than its diff:
```python
import functools

import jax
import jax.numpy as jnp
from jax import lax
from jax.experimental import pallas as pl
from jax.experimental.pallas import tpu as pltpu
from jax.sharding import PartitionSpec as P

MESH = pl.DeviceIdType.MESH

LANES = 128
BLOCK = 64
LOCAL = 16
SUB = 8
A_DIST = (8, 4, 2, 1)
B_DIST = (8, 4, 2)
N_DIST = (8, 4, 2, 1)
UP1, UP2, UP3, DOWN1, DOWN2, DOWN3 = range(6)


def gelu(x):
    return 0.5 * x * (1.0 + lax.erf(x * (0.5**0.5)))


def run_stages(buf, c, weights, stage0, dists, last=None):
    for step, dist in enumerate(dists):
        for low in range(LOCAL):
            if low & dist:
                continue
            high = low + dist
            act = jnp.concatenate([buf[c, low], buf[c, high]], axis=0)
            mat = jnp.concatenate([weights[stage0 + step, low], weights[stage0 + step, high]], axis=0)
            mixed = jnp.dot(mat, act, preferred_element_type=jnp.float32)
            if last is not None and step == len(dists) - 1:
                mixed = last(mixed.astype(jnp.bfloat16).astype(jnp.float32))
            mixed = mixed.astype(jnp.bfloat16)
            buf[c, low] = mixed[:BLOCK]
            buf[c, high] = mixed[BLOCK:]


def kernel(
    chunks,
    sig, w1, w2, out,
    inb, a1, b1, nb, b2, a2, ob,
    raw1, raw2, send_a, send_b, wa, wb, wn,
    in_sem, raw_sem, move_send, move_recv, wa_send, wa_recv, wb_send, wb_recv, out_sem,
):
    me = lax.axis_index("sp")
    zy = me // SUB
    xc = lax.rem(me, SUB)
    twist = 2 * (xc ^ 1)
    half = zy // 2
    own_l = zy ^ twist
    own_g = xc ^ half

    def device(zy_, xc_):
        return {"sp": zy_ * SUB + xc_}

    def remote(src, dst, send, recv, target):
        return pltpu.make_async_remote_copy(
            src_ref=src, dst_ref=dst, send_sem=send, recv_sem=recv, device_id=target, device_id_type=MESH
        )

    def in_copy(c):
        return pltpu.make_async_copy(sig.at[:, :, pl.ds(c * LANES, LANES)], inb.at[c], in_sem.at[c])

    def raw_copy(which, s):
        src, dst = ((w1, raw1), (w2, raw2))[which]
        return pltpu.make_async_copy(src.at[s], dst.at[s], raw_sem.at[which, s])

    def out_copy(c):
        return pltpu.make_async_copy(ob.at[c], out.at[:, :, pl.ds(c * LANES, LANES)], out_sem.at[c])


    def send_up1(c):
        def one(i, _):
            to = zy ^ i
            remote(
                inb.at[c, to ^ twist], a1.at[c, zy], move_send.at[UP1, c], move_recv.at[UP1, c], device(to, xc)
            ).start()
            return 0

        lax.fori_loop(1, LOCAL, one, 0)
        a1[c, zy] = inb[c, own_l]

    def send_up2(c):
        def one(i, _):
            q = zy ^ i
            remote(
                a1.at[c, q], b1.at[c, 2 * xc + lax.rem(own_l, 2)], move_send.at[UP2, c], move_recv.at[UP2, c],
                device(q, (own_l // 2) ^ (q // 2)),
            ).start()
            return 0

        lax.fori_loop(0, LOCAL, one, 0)

    def send_up3(c):
        def one(i, _):
            t = xc ^ i
            remote(
                b1.at[c, pl.ds(2 * t, 2)], nb.at[c, pl.ds(2 * own_g, 2)], move_send.at[UP3, c], move_recv.at[UP3, c],
                device(zy, t),
            ).start()
            return 0

        lax.fori_loop(1, SUB, one, 0)
        nb[c, pl.ds(2 * own_g, 2)] = b1[c, pl.ds(2 * xc, 2)]

    def send_down1(c):
        def one(i, _):
            to = xc ^ i
            remote(
                nb.at[c, pl.ds(2 * (to ^ half), 2)], b2.at[c, pl.ds(2 * xc, 2)], move_send.at[DOWN1, c],
                move_recv.at[DOWN1, c], device(zy, to),
            ).start()
            return 0

        lax.fori_loop(1, SUB, one, 0)
        b2[c, pl.ds(2 * xc, 2)] = nb[c, pl.ds(2 * own_g, 2)]

    def send_down2(c):
        def one(i, _):
            slot = i
            t = slot // 2
            to = (2 * own_g + lax.rem(slot, 2)) ^ (2 * (t ^ 1))
            remote(
                b2.at[c, slot], a2.at[c, zy], move_send.at[DOWN2, c], move_recv.at[DOWN2, c], device(to, t)
            ).start()
            return 0

        lax.fori_loop(0, LOCAL, one, 0)

    def send_down3(c):
        def one(i, _):
            q = zy ^ i
            remote(
                a2.at[c, q], ob.at[c, own_l], move_send.at[DOWN3, c], move_recv.at[DOWN3, c], device(q, xc)
            ).start()
            return 0

        lax.fori_loop(1, LOCAL, one, 0)
        ob[c, own_l] = a2[c, zy]

    remote_blocks = {UP1: 15, UP2: 16, UP3: 14, DOWN1: 14, DOWN2: 16, DOWN3: 15}

    def arrived(move, buf, c):
        n = remote_blocks[move]
        pltpu.make_async_copy(buf.at[c, pl.ds(0, n)], buf.at[c, pl.ds(0, n)], move_recv.at[move, c]).wait()

    def drained(move, buf, c):
        n = remote_blocks[move]
        pltpu.make_async_copy(buf.at[c, pl.ds(0, n)], buf.at[c, pl.ds(0, n)], move_send.at[move, c]).wait()


    def side_by_side(raw, s, l, bit):
        return jnp.concatenate([raw[s, l, bit], raw[s, l, 1 - bit]], axis=1)

    def send_wa(which, s, bit):
        raw = (raw1, raw2)[which]
        raw_s = s if which == 0 else 7 + s
        raw_copy(which, raw_s).wait()
        slot = 4 * which + s

        def build(l, _):
            send_a[slot, l] = side_by_side(raw, raw_s, l, bit)
            return 0

        lax.fori_loop(0, LOCAL, build, 0, unroll=4)

        def one(i, _):
            to = zy ^ i
            remote(
                send_a.at[slot, to ^ twist], wa.at[slot, zy], wa_send.at[slot], wa_recv.at[slot], device(to, xc)
            ).start()
            return 0

        lax.fori_loop(1, LOCAL, one, 0)
        wa[slot, zy] = send_a[slot, own_l]

    def send_wb(which, s, bit):
        raw = (raw1, raw2)[which]
        raw_copy(which, 4 + s).wait()
        slot = 3 * which + s

        def build(l, _):
            send_b[slot, l] = side_by_side(raw, 4 + s, l, bit)
            return 0

        lax.fori_loop(0, LOCAL, build, 0, unroll=4)

        def one(i, _):
            to = xc ^ i
            remote(
                send_b.at[slot, pl.ds(2 * (to ^ half), 2)], wb.at[slot, pl.ds(2 * xc, 2)], wb_send.at[slot],
                wb_recv.at[slot], device(zy, to),
            ).start()
            return 0

        lax.fori_loop(1, SUB, one, 0)
        wb[slot, pl.ds(2 * xc, 2)] = send_b[slot, pl.ds(2 * own_g, 2)]

    def build_wn(which, s, dist):
        raw = (raw1, raw2)[which]
        raw_s = 7 + s if which == 0 else s
        raw_copy(which, raw_s).wait()

        def build(l, _):
            wn[4 * which + s, l] = side_by_side(raw, raw_s, l, lax.rem(l // dist, 2))
            return 0

        lax.fori_loop(0, LOCAL, build, 0, unroll=4)

    def wa_arrived(slot, sem):
        pltpu.make_async_copy(wa.at[slot, pl.ds(0, 15)], wa.at[slot, pl.ds(0, 15)], sem.at[slot]).wait()

    def wb_arrived(slot, sem):
        pltpu.make_async_copy(wb.at[slot, pl.ds(0, 14)], wb.at[slot, pl.ds(0, 14)], sem.at[slot]).wait()


    in_copy(0).start()
    for s in range(4):
        raw_copy(0, s).start()
    for c in range(1, chunks):
        in_copy(c).start()
    for s in range(4, 11):
        raw_copy(0, s).start()
    for s in range(11):
        raw_copy(1, s).start()

    in_copy(0).wait()
    send_up1(0)
    for s in range(4):
        send_wa(0, s, lax.rem(zy // A_DIST[s], 2))
    in_copy(1).wait()
    send_up1(1)
    for s in range(3):
        send_wb(0, s, lax.rem(xc // (B_DIST[s] // 2), 2))
    for s in range(4):
        build_wn(0, s, N_DIST[s])
    for s in range(4):
        build_wn(1, s, N_DIST[3 - s])
    for s in range(3):
        send_wb(1, s, lax.rem(xc // (B_DIST[2 - s] // 2), 2))


    def slot_body(t, _):
        @pl.when(t < chunks)
        def _():
            @pl.when(t == 0)
            def _():
                for s in range(4):
                    wa_arrived(s, wa_recv)

            arrived(UP1, a1, t)
            run_stages(a1, t, wa, 0, A_DIST)
            send_up2(t)

            @pl.when(t + 2 < chunks)
            def _():
                in_copy(t + 2).wait()
                send_up1(t + 2)

            @pl.when(t == 0)
            def _():
                for s in range(4):
                    send_wa(1, s, lax.rem(zy // A_DIST[3 - s], 2))

        c1 = t - 1

        @pl.when((c1 >= 0) & (c1 < chunks))
        def _():
            @pl.when(c1 == 0)
            def _():
                for s in range(3):
                    wb_arrived(s, wb_recv)

            arrived(UP2, b1, c1)
            run_stages(b1, c1, wb, 0, B_DIST)
            send_up3(c1)

        c2 = t - 2

        @pl.when((c2 >= 0) & (c2 < chunks))
        def _():
            arrived(UP3, nb, c2)
            run_stages(nb, c2, wn, 0, N_DIST, last=gelu)
            run_stages(nb, c2, wn, 4, N_DIST[::-1])
            send_down1(c2)

        c3 = t - 3

        @pl.when((c3 >= 0) & (c3 < chunks))
        def _():
            @pl.when(c3 == 0)
            def _():
                for s in range(3):
                    wb_arrived(3 + s, wb_recv)

            arrived(DOWN1, b2, c3)
            run_stages(b2, c3, wb, 3, B_DIST[::-1])
            send_down2(c3)

        c4 = t - 4

        @pl.when((c4 >= 0) & (c4 < chunks))
        def _():
            @pl.when(c4 == 0)
            def _():
                for s in range(4):
                    wa_arrived(4 + s, wa_recv)

            arrived(DOWN2, a2, c4)
            run_stages(a2, c4, wa, 4, A_DIST[::-1])
            send_down3(c4)

        c5 = t - 5

        @pl.when(c5 >= 0)
        def _():
            arrived(DOWN3, ob, c5)
            out_copy(c5).start()

        return 0

    lax.fori_loop(0, chunks + 5, slot_body, 0)

    def finish(c, _):
        out_copy(c).wait()
        drained(UP1, inb, c)
        drained(UP2, a1, c)
        drained(UP3, b1, c)
        drained(DOWN1, nb, c)
        drained(DOWN2, b2, c)
        drained(DOWN3, a2, c)
        return 0

    lax.fori_loop(0, chunks, finish, 0)
    for slot in range(8):
        wa_arrived(slot, wa_send)
    for slot in range(6):
        wb_arrived(slot, wb_send)


def solution(mesh):
    def device_program(signal, w_first, w_second):
        rows, columns = signal.shape
        stages = w_first.shape[0]
        chunks = columns // LANES
        bf16 = jnp.bfloat16
        moved = pltpu.VMEM((chunks, LOCAL, BLOCK, LANES), bf16)
        raw = pltpu.VMEM((stages, LOCAL, 2, BLOCK, BLOCK), bf16)

        def paired(n):
            return pltpu.VMEM((n, LOCAL, BLOCK, LANES), bf16)

        dma = pltpu.SemaphoreType.DMA
        hbm = pl.BlockSpec(memory_space=pl.ANY)
        result = pl.pallas_call(
            functools.partial(kernel, chunks),
            out_shape=jax.ShapeDtypeStruct((LOCAL, BLOCK, columns), bf16),
            in_specs=[hbm, hbm, hbm],
            out_specs=hbm,
            scratch_shapes=[moved] * 7
            + [raw, raw, paired(8), paired(6), paired(8), paired(6), paired(8)]
            + [
                dma((chunks,)),
                dma((2, stages)),
                dma((6, chunks)),
                dma((6, chunks)),
                dma((8,)),
                dma((8,)),
                dma((6,)),
                dma((6,)),
                dma((chunks,)),
            ],
            compiler_params=pltpu.CompilerParams(has_side_effects=True, vmem_limit_bytes=60 * 2**20),
        )(signal.reshape(LOCAL, BLOCK, columns), w_first, w_second)
        return result.reshape(rows, columns)

    row_spec = P(("dp", "sp"), None)
    weight_spec = P(None, "sp", None, None, None)
    return jax.shard_map(
        device_program, mesh=mesh, in_specs=(row_spec, weight_spec, weight_spec), out_specs=row_spec, check_vma=False
    )
```

time: 635 us -> 163 us (0.26); the launches traced: 623 us -> 163 us
  waiting for transfers between devices: 518 us -> 0 us
  Pallas kernels: 0 us -> 160 us
  matrix products: 49.7 us -> 0 us
  starting transfers between devices: 29.6 us -> 0 us
  local copies, waits for them, and re-layouts: 25.1 us -> 3.08 us
    ppermute x14 -> x0, waiting for transfers between devices: 518 us -> none  [apply_map(): partner = lax.ppermute(act_blocks, 'sp', pairing)]
    pallas_call x0 -> x1, Pallas kernels: none -> 160 us  [device_program(): pl.pallas_call(functools.partial(kernel, chunks), out_shape=jax.ShapeDtyp...]
    dot_general x44 -> x0, matrix products: 49.7 us -> none  [the longest x22 25.8 us: mix_blocks(): jnp.einsum('lij,ljc->lic', weights[:, 1], partner, preferred_element_type...]
    ppermute x14 -> x0, starting transfers between devices: 29.6 us -> none  [apply_map(): partner = lax.ppermute(act_blocks, 'sp', pairing)]
    rev x8 -> x0, local copies, waits for them, and re-layouts: 12.7 us -> none  [local_partner(): return grouped[:, ::-1].reshape(act_blocks.shape)]
    slice x2 -> x0, local copies, waits for them, and re-layouts: 6.71 us -> none  [apply_map(): act_blocks = mix_blocks(act_blocks, partner, weights[stage])]
  transfers between devices with their start and end apart: 14 -> 0, of which waited for: 13 -> 0; matrix products, arithmetic and copies ran while one was open for 3% -> 0% of each run, Pallas kernels for 0% -> 0%
where the time goes in v1:
time: 163 us
  Pallas kernels  160 us (98%)
  local copies, waits for them, and re-layouts  3.08 us (2%)
    pallas_call x1, Pallas kernels, device_program(): pl.pallas_call(functools.partial(kernel, chunks), out_shape=jax.ShapeDtyp...  160 us

profile of v1, /device:TPU:1, one launch (start us, length us, event | category | flops | bytes accessed | tf_op | source)
XLA Modules:
  0.0 162.6 jit_solution(13104664662323925805)
XLA Ops:
  0.0 159.5 %shard_map.37 = bf16[16,64,1024]{2,1,0:T(8,128)(2,1)} custom-call(bf16[16,64,1024]{2,1,0:T(8,128)(2,1)} %bitcast.3, bf16[11,16,2,64,64]{4,3,2,1,0:T(8,128)(2,1)} %w1.1, bf16[11,16,2,64,64]{4,3,2,1,0:T(8,128)(2,1)} %w2.1), custom_call_target="tpu_custom_call" | custom-call | tf_op jit(solution)/shard_map/pallas_call | solution.py:359
  159.5 3.1 %copy.5 = bf16[1024,1024]{1,0:T(8,128)(2,1)} copy(bf16[1024,1024]{1,0:T(8,128)(2,1)} %bitcast.2) | data formatting | bytes 4194304

commit v2 on v1

--- a/solution.py
+++ b/solution.py
@@ -17,6 +17,13 @@
 B_DIST = (8, 4, 2)
 N_DIST = (8, 4, 2, 1)
 UP1, UP2, UP3, DOWN1, DOWN2, DOWN3 = range(6)
+AT_A1, AT_B1, AT_N, AT_B2, AT_A2, AT_OUT = 0, 2, 4, 6, 8, 10
+AHEAD = 3
+AT_WA2 = 5
+
+
+def swap(v):
+    return lax.rem(v, 2) + 2 * (v // 4) + 4 * lax.rem(v // 2, 2)
 
 
 def gelu(x):
@@ -49,10 +56,10 @@
     me = lax.axis_index("sp")
     zy = me // SUB
     xc = lax.rem(me, SUB)
-    twist = 2 * (xc ^ 1)
+    twist = 2 * swap(xc ^ 7)
     half = zy // 2
     own_l = zy ^ twist
-    own_g = xc ^ half
+    own_h = swap(xc) ^ half
 
     def device(zy_, xc_):
         return {"sp": zy_ * SUB + xc_}
@@ -89,7 +96,7 @@
             q = zy ^ i
             remote(
                 a1.at[c, q], b1.at[c, 2 * xc + lax.rem(own_l, 2)], move_send.at[UP2, c], move_recv.at[UP2, c],
-                device(q, (own_l // 2) ^ (q // 2)),
+                device(q, swap((own_l // 2) ^ (q // 2))),
             ).start()
             return 0
 
@@ -99,31 +106,31 @@
         def one(i, _):
             t = xc ^ i
             remote(
-                b1.at[c, pl.ds(2 * t, 2)], nb.at[c, pl.ds(2 * own_g, 2)], move_send.at[UP3, c], move_recv.at[UP3, c],
+                b1.at[c, pl.ds(2 * t, 2)], nb.at[c, pl.ds(2 * own_h, 2)], move_send.at[UP3, c], move_recv.at[UP3, c],
                 device(zy, t),
             ).start()
             return 0
 
         lax.fori_loop(1, SUB, one, 0)
-        nb[c, pl.ds(2 * own_g, 2)] = b1[c, pl.ds(2 * xc, 2)]
+        nb[c, pl.ds(2 * own_h, 2)] = b1[c, pl.ds(2 * xc, 2)]
 
     def send_down1(c):
         def one(i, _):
             to = xc ^ i
             remote(
-                nb.at[c, pl.ds(2 * (to ^ half), 2)], b2.at[c, pl.ds(2 * xc, 2)], move_send.at[DOWN1, c],
+                nb.at[c, pl.ds(2 * (swap(to) ^ half), 2)], b2.at[c, pl.ds(2 * xc, 2)], move_send.at[DOWN1, c],
                 move_recv.at[DOWN1, c], device(zy, to),
             ).start()
             return 0
 
         lax.fori_loop(1, SUB, one, 0)
-        b2[c, pl.ds(2 * xc, 2)] = nb[c, pl.ds(2 * own_g, 2)]
+        b2[c, pl.ds(2 * xc, 2)] = nb[c, pl.ds(2 * own_h, 2)]
 
     def send_down2(c):
         def one(i, _):
-            slot = i
-            t = slot // 2
-            to = (2 * own_g + lax.rem(slot, 2)) ^ (2 * (t ^ 1))
+            t = xc ^ (i // 2)
+            slot = 2 * t + lax.rem(i, 2)
+            to = (2 * own_h + lax.rem(i, 2)) ^ (2 * swap(t ^ 7))
             remote(
                 b2.at[c, slot], a2.at[c, zy], move_send.at[DOWN2, c], move_recv.at[DOWN2, c], device(to, t)
             ).start()
@@ -156,7 +163,7 @@
     def side_by_side(raw, s, l, bit):
         return jnp.concatenate([raw[s, l, bit], raw[s, l, 1 - bit]], axis=1)
 
-    def send_wa(which, s, bit):
+    def build_wa(which, s, bit):
         raw = (raw1, raw2)[which]
         raw_s = s if which == 0 else 7 + s
         raw_copy(which, raw_s).wait()
@@ -168,6 +175,9 @@
 
         lax.fori_loop(0, LOCAL, build, 0, unroll=4)
 
+    def send_wa(which, s):
+        slot = 4 * which + s
+
         def one(i, _):
             to = zy ^ i
             remote(
@@ -192,13 +202,13 @@
         def one(i, _):
             to = xc ^ i
             remote(
-                send_b.at[slot, pl.ds(2 * (to ^ half), 2)], wb.at[slot, pl.ds(2 * xc, 2)], wb_send.at[slot],
+                send_b.at[slot, pl.ds(2 * (swap(to) ^ half), 2)], wb.at[slot, pl.ds(2 * xc, 2)], wb_send.at[slot],
                 wb_recv.at[slot], device(zy, to),
             ).start()
             return 0
 
         lax.fori_loop(1, SUB, one, 0)
-        wb[slot, pl.ds(2 * xc, 2)] = send_b[slot, pl.ds(2 * own_g, 2)]
+        wb[slot, pl.ds(2 * xc, 2)] = send_b[slot, pl.ds(2 * own_h, 2)]
 
     def build_wn(which, s, dist):
         raw = (raw1, raw2)[which]
@@ -228,12 +238,40 @@
     for s in range(11):
         raw_copy(1, s).start()
 
+
+    barrier = pltpu.get_barrier_semaphore()
+
+    def greet(target):
+        pl.semaphore_signal(barrier, inc=1, device_id=target, device_id_type=MESH)
+
+    def greet_zy(i, _):
+        greet(device(zy ^ i, xc))
+        return 0
+
+    def greet_xc(i, _):
+        greet(device(zy, xc ^ i))
+        return 0
+
+    def greet_all(q, _):
+        greet(device(q, swap((own_l // 2) ^ (q // 2))))
+        t = q // 2
+        greet(device((2 * own_h + lax.rem(q, 2)) ^ (2 * swap(t ^ 7)), t))
+        return 0
+
+    lax.fori_loop(1, LOCAL, greet_zy, 0)
+    lax.fori_loop(1, SUB, greet_xc, 0)
+    lax.fori_loop(0, LOCAL, greet_all, 0)
+    for s in range(4):
+        build_wa(0, s, lax.rem(zy // A_DIST[s], 2))
     in_copy(0).wait()
+    pl.semaphore_wait(barrier, 15 + 7 + 32)
+
     send_up1(0)
     for s in range(4):
-        send_wa(0, s, lax.rem(zy // A_DIST[s], 2))
-    in_copy(1).wait()
-    send_up1(1)
+        send_wa(0, s)
+    for c in range(1, AHEAD):
+        in_copy(c).wait()
+        send_up1(c)
     for s in range(3):
         send_wb(0, s, lax.rem(xc // (B_DIST[s] // 2), 2))
     for s in range(4):
@@ -244,86 +282,95 @@
         send_wb(1, s, lax.rem(xc // (B_DIST[2 - s] // 2), 2))
 
 
+    def at(c, body):
+        pl.when((c >= 0) & (c < chunks))(body)
+
     def slot_body(t, _):
-        @pl.when(t < chunks)
-        def _():
-            @pl.when(t == 0)
+        def first_a():
+            c = t - AT_A1
+
+            @pl.when(c == 0)
             def _():
                 for s in range(4):
                     wa_arrived(s, wa_recv)
 
-            arrived(UP1, a1, t)
-            run_stages(a1, t, wa, 0, A_DIST)
-            send_up2(t)
-
-            @pl.when(t + 2 < chunks)
-            def _():
-                in_copy(t + 2).wait()
-                send_up1(t + 2)
-
-            @pl.when(t == 0)
-            def _():
-                for s in range(4):
-                    send_wa(1, s, lax.rem(zy // A_DIST[3 - s], 2))
-
-        c1 = t - 1
-
-        @pl.when((c1 >= 0) & (c1 < chunks))
+            arrived(UP1, a1, c)
+            run_stages(a1, c, wa, 0, A_DIST)
+            send_up2(c)
+
+        at(t - AT_A1, first_a)
+
+        @pl.when(t + AHEAD < chunks)
         def _():
-            @pl.when(c1 == 0)
+            in_copy(t + AHEAD).wait()
+            send_up1(t + AHEAD)
+
+        @pl.when(t == AT_WA2)
+        def _():
+            for s in range(4):
+                build_wa(1, s, lax.rem(zy // A_DIST[3 - s], 2))
+                send_wa(1, s)
+
+        def first_b():
+            c = t - AT_B1
+
+            @pl.when(c == 0)
             def _():
                 for s in range(3):
                     wb_arrived(s, wb_recv)
 
-            arrived(UP2, b1, c1)
-            run_stages(b1, c1, wb, 0, B_DIST)
-            send_up3(c1)
-
-        c2 = t - 2
-
-        @pl.when((c2 >= 0) & (c2 < chunks))
-        def _():
-            arrived(UP3, nb, c2)
-            run_stages(nb, c2, wn, 0, N_DIST, last=gelu)
-            run_stages(nb, c2, wn, 4, N_DIST[::-1])
-            send_down1(c2)
-
-        c3 = t - 3
-
-        @pl.when((c3 >= 0) & (c3 < chunks))
-        def _():
-            @pl.when(c3 == 0)
+            arrived(UP2, b1, c)
+            run_stages(b1, c, wb, 0, B_DIST)
+            send_up3(c)
+
+        at(t - AT_B1, first_b)
+
+        def middle():
+            c = t - AT_N
+            arrived(UP3, nb, c)
+            run_stages(nb, c, wn, 0, N_DIST, last=gelu)
+            run_stages(nb, c, wn, 4, N_DIST[::-1])
+            send_down1(c)
+
+        at(t - AT_N, middle)
+
+        def second_b():
+            c = t - AT_B2
+
+            @pl.when(c == 0)
             def _():
                 for s in range(3):
                     wb_arrived(3 + s, wb_recv)
 
-            arrived(DOWN1, b2, c3)
-            run_stages(b2, c3, wb, 3, B_DIST[::-1])
-            send_down2(c3)
-
-        c4 = t - 4
-
-        @pl.when((c4 >= 0) & (c4 < chunks))
-        def _():
-            @pl.when(c4 == 0)
+            arrived(DOWN1, b2, c)
+            run_stages(b2, c, wb, 3, B_DIST[::-1])
+            send_down2(c)
+
+        at(t - AT_B2, second_b)
+
+        def second_a():
+            c = t - AT_A2
+
+            @pl.when(c == 0)
             def _():
                 for s in range(4):
                     wa_arrived(4 + s, wa_recv)
 
-            arrived(DOWN2, a2, c4)
-            run_stages(a2, c4, wa, 4, A_DIST[::-1])
-            send_down3(c4)
-
-        c5 = t - 5
-
-        @pl.when(c5 >= 0)
-        def _():
-            arrived(DOWN3, ob, c5)
-            out_copy(c5).start()
-
+            arrived(DOWN2, a2, c)
+            run_stages(a2, c, wa, 4, A_DIST[::-1])
+            send_down3(c)
+
+        at(t - AT_A2, second_a)
+
+        def store():
+            c = t - AT_OUT
+            arrived(DOWN3, ob, c)
+            out_copy(c).start()
+
+        at(t - AT_OUT, store)
         return 0
 
-    lax.fori_loop(0, chunks + 5, slot_body, 0)
+    lax.fori_loop(0, chunks + AT_OUT, slot_body, 0)
 
     def finish(c, _):
         out_copy(c).wait()
@@ -374,7 +421,9 @@
                 dma((6,)),
                 dma((chunks,)),
             ],
-            compiler_params=pltpu.CompilerParams(has_side_effects=True, vmem_limit_bytes=60 * 2**20),
+            compiler_params=pltpu.CompilerParams(
+                collective_id=0, has_side_effects=True, vmem_limit_bytes=60 * 2**20
+            ),
         )(signal.reshape(LOCAL, BLOCK, columns), w_first, w_second)
         return result.reshape(rows, columns)
 

time: 163 us -> 146 us (0.90)
  Pallas kernels: 160 us -> 143 us
    pallas_call x1, Pallas kernels: 160 us -> 143 us  [device_program(): pl.pallas_call(functools.partial(kernel, chunks), out_shape=jax.ShapeDtyp...]
where the time goes in v2:
time: 146 us
  Pallas kernels  143 us (98%)
  local copies, waits for them, and re-layouts  3.08 us (2%)
    pallas_call x1, Pallas kernels, device_program(): pl.pallas_call(functools.partial(kernel, chunks), out_shape=jax.ShapeDtyp...  143 us
    unnamed x1, local copies, waits for them, and re-layouts  3.08 us

profile of v2, /device:TPU:1, one launch (start us, length us, event | category | flops | bytes accessed | tf_op | source)
XLA Modules:
  0.0 146.0 jit_solution(17685333161944187992)
XLA Ops:
  0.0 142.9 %shard_map.37 = bf16[16,64,1024]{2,1,0:T(8,128)(2,1)} custom-call(bf16[16,64,1024]{2,1,0:T(8,128)(2,1)} %bitcast.3, bf16[11,16,2,64,64]{4,3,2,1,0:T(8,128)(2,1)} %w1.1, bf16[11,16,2,64,64]{4,3,2,1,0:T(8,128)(2,1)} %w2.1), custom_call_target="tpu_custom_call" | custom-call | tf_op jit(solution)/shard_map/pallas_call | solution.py:406
  142.9 3.1 %copy.5 = bf16[1024,1024]{1,0:T(8,128)(2,1)} copy(bf16[1024,1024]{1,0:T(8,128)(2,1)} %bitcast.2) | data formatting | bytes 4194304

commit v3 on v2

--- a/solution.py
+++ b/solution.py
@@ -11,6 +11,7 @@
 
 LANES = 128
 BLOCK = 64
+HALF = 32
 LOCAL = 16
 SUB = 8
 A_DIST = (8, 4, 2, 1)
@@ -48,8 +49,8 @@
 
 def kernel(
     chunks,
-    sig, w1, w2, out,
-    inb, a1, b1, nb, b2, a2, ob,
+    sig, w1, w2, ob,
+    inb, a1, b1, nb, b2, a2,
     raw1, raw2, send_a, send_b, wa, wb, wn,
     in_sem, raw_sem, move_send, move_recv, wa_send, wa_recv, wb_send, wb_recv, out_sem,
 ):
@@ -77,18 +78,20 @@
         return pltpu.make_async_copy(src.at[s], dst.at[s], raw_sem.at[which, s])
 
     def out_copy(c):
-        return pltpu.make_async_copy(ob.at[c], out.at[:, :, pl.ds(c * LANES, LANES)], out_sem.at[c])
+        return pltpu.make_async_copy(a2.at[c, zy], ob.at[c, own_l], out_sem.at[c])
 
 
     def send_up1(c):
         def one(i, _):
-            to = zy ^ i
-            remote(
-                inb.at[c, to ^ twist], a1.at[c, zy], move_send.at[UP1, c], move_recv.at[UP1, c], device(to, xc)
-            ).start()
-            return 0
-
-        lax.fori_loop(1, LOCAL, one, 0)
+            to = zy ^ (1 + lax.rem(i, LOCAL - 1))
+            rows = pl.ds((i // (LOCAL - 1)) * HALF, HALF)
+            remote(
+                inb.at[c, to ^ twist, rows], a1.at[c, zy, rows], move_send.at[UP1, c], move_recv.at[UP1, c],
+                device(to, xc),
+            ).start()
+            return 0
+
+        lax.fori_loop(0, 2 * (LOCAL - 1), one, 0)
         a1[c, zy] = inb[c, own_l]
 
     def send_up2(c):
@@ -140,14 +143,16 @@
 
     def send_down3(c):
         def one(i, _):
-            q = zy ^ i
-            remote(
-                a2.at[c, q], ob.at[c, own_l], move_send.at[DOWN3, c], move_recv.at[DOWN3, c], device(q, xc)
-            ).start()
-            return 0
-
-        lax.fori_loop(1, LOCAL, one, 0)
-        ob[c, own_l] = a2[c, zy]
+            q = zy ^ (1 + lax.rem(i, LOCAL - 1))
+            rows = pl.ds((i // (LOCAL - 1)) * HALF, HALF)
+            remote(
+                a2.at[c, q, rows], ob.at[c, own_l, rows], move_send.at[DOWN3, c], move_recv.at[DOWN3, c],
+                device(q, xc),
+            ).start()
+            return 0
+
+        lax.fori_loop(0, 2 * (LOCAL - 1), one, 0)
+        out_copy(c).start()
 
     remote_blocks = {UP1: 15, UP2: 16, UP3: 14, DOWN1: 14, DOWN2: 16, DOWN3: 15}
 
@@ -179,13 +184,15 @@
         slot = 4 * which + s
 
         def one(i, _):
-            to = zy ^ i
-            remote(
-                send_a.at[slot, to ^ twist], wa.at[slot, zy], wa_send.at[slot], wa_recv.at[slot], device(to, xc)
-            ).start()
-            return 0
-
-        lax.fori_loop(1, LOCAL, one, 0)
+            to = zy ^ (1 + lax.rem(i, LOCAL - 1))
+            rows = pl.ds((i // (LOCAL - 1)) * HALF, HALF)
+            remote(
+                send_a.at[slot, to ^ twist, rows], wa.at[slot, zy, rows], wa_send.at[slot], wa_recv.at[slot],
+                device(to, xc),
+            ).start()
+            return 0
+
+        lax.fori_loop(0, 2 * (LOCAL - 1), one, 0)
         wa[slot, zy] = send_a[slot, own_l]
 
     def send_wb(which, s, bit):
@@ -365,7 +372,6 @@
         def store():
             c = t - AT_OUT
             arrived(DOWN3, ob, c)
-            out_copy(c).start()
 
         at(t - AT_OUT, store)
         return 0
@@ -389,6 +395,20 @@
         wb_arrived(slot, wb_send)
 
 
+def gather_chunks(chunks, parts, out, buf, in_sem, out_sem):
+    into = [pltpu.make_async_copy(parts.at[c], buf.at[c], in_sem.at[c]) for c in range(chunks)]
+    onto = [
+        pltpu.make_async_copy(buf.at[c], out.at[:, pl.ds(c * LANES, LANES)], out_sem.at[c]) for c in range(chunks)
+    ]
+    for copy in into:
+        copy.start()
+    for c in range(chunks):
+        into[c].wait()
+        onto[c].start()
+    for copy in onto:
+        copy.wait()
+
+
 def solution(mesh):
     def device_program(signal, w_first, w_second):
         rows, columns = signal.shape
@@ -405,10 +425,10 @@
         hbm = pl.BlockSpec(memory_space=pl.ANY)
         result = pl.pallas_call(
             functools.partial(kernel, chunks),
-            out_shape=jax.ShapeDtypeStruct((LOCAL, BLOCK, columns), bf16),
+            out_shape=jax.ShapeDtypeStruct((chunks, LOCAL, BLOCK, LANES), bf16),
             in_specs=[hbm, hbm, hbm],
             out_specs=hbm,
-            scratch_shapes=[moved] * 7
+            scratch_shapes=[moved] * 6
             + [raw, raw, paired(8), paired(6), paired(8), paired(6), paired(8)]
             + [
                 dma((chunks,)),
@@ -425,7 +445,14 @@
                 collective_id=0, has_side_effects=True, vmem_limit_bytes=60 * 2**20
             ),
         )(signal.reshape(LOCAL, BLOCK, columns), w_first, w_second)
-        return result.reshape(rows, columns)
+        return pl.pallas_call(
+            functools.partial(gather_chunks, chunks),
+            out_shape=jax.ShapeDtypeStruct((rows, columns), bf16),
+            in_specs=[hbm],
+            out_specs=hbm,
+            scratch_shapes=[pltpu.VMEM((chunks, rows, LANES), bf16), dma((chunks,)), dma((chunks,))],
+            compiler_params=pltpu.CompilerParams(vmem_limit_bytes=60 * 2**20),
+        )(result.reshape(chunks, rows, LANES))
 
     row_spec = P(("dp", "sp"), None)
     weight_spec = P(None, "sp", None, None, None)

time: 146 us -> 143 us (0.979)
  local copies, waits for them, and re-layouts: 3.08 us -> 0 us
    unnamed x1 -> x0, local copies, waits for them, and re-layouts: 3.08 us -> none
    pallas_call x0 -> x1, Pallas kernels: none -> 2.4 us  [device_program(): pl.pallas_call(functools.partial(gather_chunks, chunks), out_shape=jax.Sh...]
    pallas_call x1, Pallas kernels: 143 us -> 141 us  [device_program(): pl.pallas_call(functools.partial(kernel, chunks), out_shape=jax.ShapeDtyp...]
where the time goes in v3:
time: 143 us
  Pallas kernels  143 us (100%)
    pallas_call x1, Pallas kernels, device_program(): pl.pallas_call(functools.partial(kernel, chunks), out_shape=jax.ShapeDtyp...  141 us

profile of v3, /device:TPU:1, one launch (start us, length us, event | category | flops | bytes accessed | tf_op | source)
XLA Modules:
  0.0 143.3 jit_solution(13629350665871497432)
XLA Ops:
  0.0 140.9 %shard_map.37 = bf16[8,16,64,128]{3,2,1,0:T(8,128)(2,1)} custom-call(bf16[16,64,1024]{2,1,0:T(8,128)(2,1)} %bitcast.3, bf16[11,16,2,64,64]{4,3,2,1,0:T(8,128)(2,1)} %w1.1, bf16[11,16,2,64,64]{4,3,2,1,0:T(8,128)(2,1)} %w2.1), custom_call_target="tpu_custom_call" | custom-call | tf_op jit(solution)/shard_map/pallas_call | solution.py:426
  140.9 2.4 %shard_map.38 = bf16[1024,1024]{1,0:T(8,128)(2,1)} custom-call(bf16[8,1024,128]{2,1,0:T(8,128)(2,1)} %bitcast.2), custom_call_target="tpu_custom_call" | custom-call | tf_op jit(solution)/shard_map/pallas_call | solution.py:448

commit v4 on v3

--- a/solution.py
+++ b/solution.py
@@ -18,13 +18,17 @@
 B_DIST = (8, 4, 2)
 N_DIST = (8, 4, 2, 1)
 UP1, UP2, UP3, DOWN1, DOWN2, DOWN3 = range(6)
-AT_A1, AT_B1, AT_N, AT_B2, AT_A2, AT_OUT = 0, 2, 4, 6, 8, 10
+AT_A1, AT_B1, AT_N, AT_B2, AT_A2 = 0, 2, 4, 6, 8
 AHEAD = 3
-AT_WA2 = 5
+AT_WA2 = 3
 
 
 def swap(v):
     return lax.rem(v, 2) + 2 * (v // 4) + 4 * lax.rem(v // 2, 2)
+
+
+def spread(i):
+    return (15 * lax.rem(i, 2)) ^ (5 * lax.rem(i // 2, 2)) ^ (3 * lax.rem(i // 4, 2)) ^ (i // 8)
 
 
 def gelu(x):
@@ -77,7 +81,7 @@
         src, dst = ((w1, raw1), (w2, raw2))[which]
         return pltpu.make_async_copy(src.at[s], dst.at[s], raw_sem.at[which, s])
 
-    def out_copy(c):
+    def own_copy(c):
         return pltpu.make_async_copy(a2.at[c, zy], ob.at[c, own_l], out_sem.at[c])
 
 
@@ -96,14 +100,15 @@
 
     def send_up2(c):
         def one(i, _):
-            q = zy ^ i
-            remote(
-                a1.at[c, q], b1.at[c, 2 * xc + lax.rem(own_l, 2)], move_send.at[UP2, c], move_recv.at[UP2, c],
-                device(q, swap((own_l // 2) ^ (q // 2))),
-            ).start()
-            return 0
-
-        lax.fori_loop(0, LOCAL, one, 0)
+            q = zy ^ spread(lax.rem(i, LOCAL))
+            rows = pl.ds((i // LOCAL) * HALF, HALF)
+            remote(
+                a1.at[c, q, rows], b1.at[c, 2 * xc + lax.rem(own_l, 2), rows], move_send.at[UP2, c],
+                move_recv.at[UP2, c], device(q, swap((own_l // 2) ^ (q // 2))),
+            ).start()
+            return 0
+
+        lax.fori_loop(0, 2 * LOCAL, one, 0)
 
     def send_up3(c):
         def one(i, _):
@@ -131,15 +136,16 @@
 
     def send_down2(c):
         def one(i, _):
-            t = xc ^ (i // 2)
-            slot = 2 * t + lax.rem(i, 2)
-            to = (2 * own_h + lax.rem(i, 2)) ^ (2 * swap(t ^ 7))
-            remote(
-                b2.at[c, slot], a2.at[c, zy], move_send.at[DOWN2, c], move_recv.at[DOWN2, c], device(to, t)
-            ).start()
-            return 0
-
-        lax.fori_loop(0, LOCAL, one, 0)
+            step = spread(lax.rem(i, LOCAL))
+            to, t = zy ^ step, xc ^ swap(step // 2) ^ 7
+            rows = pl.ds((i // LOCAL) * HALF, HALF)
+            remote(
+                b2.at[c, 2 * t + lax.rem(to, 2), rows], a2.at[c, zy, rows], move_send.at[DOWN2, c],
+                move_recv.at[DOWN2, c], device(to, t),
+            ).start()
+            return 0
+
+        lax.fori_loop(0, 2 * LOCAL, one, 0)
 
     def send_down3(c):
         def one(i, _):
@@ -152,7 +158,7 @@
             return 0
 
         lax.fori_loop(0, 2 * (LOCAL - 1), one, 0)
-        out_copy(c).start()
+        own_copy(c).start()
 
     remote_blocks = {UP1: 15, UP2: 16, UP3: 14, DOWN1: 14, DOWN2: 16, DOWN3: 15}
 
@@ -259,22 +265,14 @@
         greet(device(zy, xc ^ i))
         return 0
 
-    def greet_all(q, _):
-        greet(device(q, swap((own_l // 2) ^ (q // 2))))
-        t = q // 2
-        greet(device((2 * own_h + lax.rem(q, 2)) ^ (2 * swap(t ^ 7)), t))
-        return 0
-
     lax.fori_loop(1, LOCAL, greet_zy, 0)
     lax.fori_loop(1, SUB, greet_xc, 0)
-    lax.fori_loop(0, LOCAL, greet_all, 0)
+    in_copy(0).wait()
+    pl.semaphore_wait(barrier, 15 + 7)
+
+    send_up1(0)
     for s in range(4):
         build_wa(0, s, lax.rem(zy // A_DIST[s], 2))
-    in_copy(0).wait()
-    pl.semaphore_wait(barrier, 15 + 7 + 32)
-
-    send_up1(0)
-    for s in range(4):
         send_wa(0, s)
     for c in range(1, AHEAD):
         in_copy(c).wait()
@@ -288,6 +286,9 @@
     for s in range(3):
         send_wb(1, s, lax.rem(xc // (B_DIST[2 - s] // 2), 2))
 
+    for s in range(3):
+        wb_arrived(s, wb_recv)
+
 
     def at(c, body):
         pl.when((c >= 0) & (c < chunks))(body)
@@ -312,19 +313,15 @@
             in_copy(t + AHEAD).wait()
             send_up1(t + AHEAD)
 
-        @pl.when(t == AT_WA2)
-        def _():
-            for s in range(4):
+        for s in range(4):
+
+            @pl.when(t == AT_WA2 + s)
+            def _(s=s):
                 build_wa(1, s, lax.rem(zy // A_DIST[3 - s], 2))
                 send_wa(1, s)
 
         def first_b():
             c = t - AT_B1
-
-            @pl.when(c == 0)
-            def _():
-                for s in range(3):
-                    wb_arrived(s, wb_recv)
 
             arrived(UP2, b1, c)
             run_stages(b1, c, wb, 0, B_DIST)
@@ -369,30 +366,31 @@
 
         at(t - AT_A2, second_a)
 
-        def store():
-            c = t - AT_OUT
-            arrived(DOWN3, ob, c)
-
-        at(t - AT_OUT, store)
         return 0
 
-    lax.fori_loop(0, chunks + AT_OUT, slot_body, 0)
+    lax.fori_loop(0, chunks + AT_A2, slot_body, 0)
 
     def finish(c, _):
-        out_copy(c).wait()
         drained(UP1, inb, c)
         drained(UP2, a1, c)
         drained(UP3, b1, c)
         drained(DOWN1, nb, c)
         drained(DOWN2, b2, c)
         drained(DOWN3, a2, c)
+        own_copy(c).wait()
         return 0
 
-    lax.fori_loop(0, chunks, finish, 0)
     for slot in range(8):
         wa_arrived(slot, wa_send)
     for slot in range(6):
         wb_arrived(slot, wb_send)
+    lax.fori_loop(0, chunks, finish, 0)
+
+    def landed(c, _):
+        arrived(DOWN3, ob, c)
+        return 0
+
+    lax.fori_loop(0, chunks, landed, 0)
 
 
 def gather_chunks(chunks, parts, out, buf, in_sem, out_sem):

time: 143 us -> 141 us (0.986)
  Pallas kernels: 143 us -> 140 us
    pallas_call x1, Pallas kernels: 141 us -> 138 us  [device_program(): pl.pallas_call(functools.partial(kernel, chunks), out_shape=jax.ShapeDtyp...]
where the time goes in v4:
time: 141 us
  Pallas kernels  140 us (99%)
    pallas_call x1, Pallas kernels, device_program(): pl.pallas_call(functools.partial(kernel, chunks), out_shape=jax.ShapeDtyp...  138 us

profile of v4, /device:TPU:1, one launch (start us, length us, event | category | flops | bytes accessed | tf_op | source)
XLA Modules:
  0.0 140.5 jit_solution(3067295018670079434)
XLA Ops:
  0.0 138.1 %shard_map.37 = bf16[8,16,64,128]{3,2,1,0:T(8,128)(2,1)} custom-call(bf16[16,64,1024]{2,1,0:T(8,128)(2,1)} %bitcast.3, bf16[11,16,2,64,64]{4,3,2,1,0:T(8,128)(2,1)} %w1.1, bf16[11,16,2,64,64]{4,3,2,1,0:T(8,128)(2,1)} %w2.1), custom_call_target="tpu_custom_call" | custom-call | tf_op jit(solution)/shard_map/pallas_call | solution.py:424
  138.1 2.4 %shard_map.38 = bf16[1024,1024]{1,0:T(8,128)(2,1)} custom-call(bf16[8,1024,128]{2,1,0:T(8,128)(2,1)} %bitcast.2), custom_call_target="tpu_custom_call" | custom-call | tf_op jit(solution)/shard_map/pallas_call | solution.py:446

commit v5 on v4

--- a/solution.py
+++ b/solution.py
@@ -95,7 +95,7 @@
             ).start()
             return 0
 
-        lax.fori_loop(0, 2 * (LOCAL - 1), one, 0)
+        lax.fori_loop(0, 2 * (LOCAL - 1), one, 0, unroll=6)
         a1[c, zy] = inb[c, own_l]
 
     def send_up2(c):
@@ -108,7 +108,7 @@
             ).start()
             return 0
 
-        lax.fori_loop(0, 2 * LOCAL, one, 0)
+        lax.fori_loop(0, 2 * LOCAL, one, 0, unroll=8)
 
     def send_up3(c):
         def one(i, _):
@@ -119,7 +119,7 @@
             ).start()
             return 0
 
-        lax.fori_loop(1, SUB, one, 0)
+        lax.fori_loop(1, SUB, one, 0, unroll=7)
         nb[c, pl.ds(2 * own_h, 2)] = b1[c, pl.ds(2 * xc, 2)]
 
     def send_down1(c):
@@ -131,7 +131,7 @@
             ).start()
             return 0
 
-        lax.fori_loop(1, SUB, one, 0)
+        lax.fori_loop(1, SUB, one, 0, unroll=7)
         b2[c, pl.ds(2 * xc, 2)] = nb[c, pl.ds(2 * own_h, 2)]
 
     def send_down2(c):
@@ -145,7 +145,7 @@
             ).start()
             return 0
 
-        lax.fori_loop(0, 2 * LOCAL, one, 0)
+        lax.fori_loop(0, 2 * LOCAL, one, 0, unroll=8)
 
     def send_down3(c):
         def one(i, _):
@@ -157,7 +157,7 @@
             ).start()
             return 0
 
-        lax.fori_loop(0, 2 * (LOCAL - 1), one, 0)
+        lax.fori_loop(0, 2 * (LOCAL - 1), one, 0, unroll=6)
         own_copy(c).start()
 
     remote_blocks = {UP1: 15, UP2: 16, UP3: 14, DOWN1: 14, DOWN2: 16, DOWN3: 15}
@@ -198,7 +198,7 @@
             ).start()
             return 0
 
-        lax.fori_loop(0, 2 * (LOCAL - 1), one, 0)
+        lax.fori_loop(0, 2 * (LOCAL - 1), one, 0, unroll=6)
         wa[slot, zy] = send_a[slot, own_l]
 
     def send_wb(which, s, bit):
@@ -220,7 +220,7 @@
             ).start()
             return 0
 
-        lax.fori_loop(1, SUB, one, 0)
+        lax.fori_loop(1, SUB, one, 0, unroll=7)
         wb[slot, pl.ds(2 * xc, 2)] = send_b[slot, pl.ds(2 * own_h, 2)]
 
     def build_wn(which, s, dist):

time: 141 us -> 139 us (0.986)
  no operation moved by 1% of the time
where the time goes in v5:
time: 139 us
  Pallas kernels  139 us (100%)
    pallas_call x1, Pallas kernels, device_program(): pl.pallas_call(functools.partial(kernel, chunks), out_shape=jax.ShapeDtyp...  137 us

profile of v5, /device:TPU:1, one launch (start us, length us, event | category | flops | bytes accessed | tf_op | source)
XLA Modules:
  0.0 139.2 jit_solution(1971168409581757664)
XLA Ops:
  0.0 136.8 %shard_map.37 = bf16[8,16,64,128]{3,2,1,0:T(8,128)(2,1)} custom-call(bf16[16,64,1024]{2,1,0:T(8,128)(2,1)} %bitcast.3, bf16[11,16,2,64,64]{4,3,2,1,0:T(8,128)(2,1)} %w1.1, bf16[11,16,2,64,64]{4,3,2,1,0:T(8,128)(2,1)} %w2.1), custom_call_target="tpu_custom_call" | custom-call | tf_op jit(solution)/shard_map/pallas_call | solution.py:424
  136.8 2.4 %shard_map.38 = bf16[1024,1024]{1,0:T(8,128)(2,1)} custom-call(bf16[8,1024,128]{2,1,0:T(8,128)(2,1)} %bitcast.2), custom_call_target="tpu_custom_call" | custom-call | tf_op jit(solution)/shard_map/pallas_call | solution.py:446

commit v6 on v5

--- a/solution.py
+++ b/solution.py
@@ -242,13 +242,15 @@
 
 
     in_copy(0).start()
-    for s in range(4):
+    for s in range(7):
         raw_copy(0, s).start()
+    for s in range(4, 7):
+        raw_copy(1, s).start()
     for c in range(1, chunks):
         in_copy(c).start()
-    for s in range(4, 11):
+    for s in range(7, 11):
         raw_copy(0, s).start()
-    for s in range(11):
+    for s in (0, 1, 2, 3, 7, 8, 9, 10):
         raw_copy(1, s).start()
 
 
@@ -274,17 +276,17 @@
     for s in range(4):
         build_wa(0, s, lax.rem(zy // A_DIST[s], 2))
         send_wa(0, s)
+        if s < 3:
+            send_wb(0, s, lax.rem(xc // (B_DIST[s] // 2), 2))
+    for s in range(3):
+        send_wb(1, s, lax.rem(xc // (B_DIST[2 - s] // 2), 2))
     for c in range(1, AHEAD):
         in_copy(c).wait()
         send_up1(c)
-    for s in range(3):
-        send_wb(0, s, lax.rem(xc // (B_DIST[s] // 2), 2))
     for s in range(4):
         build_wn(0, s, N_DIST[s])
     for s in range(4):
         build_wn(1, s, N_DIST[3 - s])
-    for s in range(3):
-        send_wb(1, s, lax.rem(xc // (B_DIST[2 - s] // 2), 2))
 
     for s in range(3):
         wb_arrived(s, wb_recv)
@@ -296,14 +298,19 @@
     def slot_body(t, _):
         def first_a():
             c = t - AT_A1
+
+            arrived(UP1, a1, c)
 
             @pl.when(c == 0)
             def _():
                 for s in range(4):
                     wa_arrived(s, wa_recv)
-
-            arrived(UP1, a1, c)
-            run_stages(a1, c, wa, 0, A_DIST)
+                    run_stages(a1, c, wa, s, (A_DIST[s],))
+
+            @pl.when(c > 0)
+            def _():
+                run_stages(a1, c, wa, 0, A_DIST)
+
             send_up2(c)
 
         at(t - AT_A1, first_a)

time: 139 us -> 139 us (level)
  no operation moved by 1% of the time
where the time goes in v6:
time: 139 us
  Pallas kernels  139 us (100%)
    pallas_call x1, Pallas kernels, device_program(): pl.pallas_call(functools.partial(kernel, chunks), out_shape=jax.ShapeDtyp...  136 us

profile of v6, /device:TPU:1, one launch (start us, length us, event | category | flops | bytes accessed | tf_op | source)
XLA Modules:
  0.0 138.8 jit_solution(12180127449499316401)
XLA Ops:
  0.0 136.4 %shard_map.37 = bf16[8,16,64,128]{3,2,1,0:T(8,128)(2,1)} custom-call(bf16[16,64,1024]{2,1,0:T(8,128)(2,1)} %bitcast.3, bf16[11,16,2,64,64]{4,3,2,1,0:T(8,128)(2,1)} %w1.1, bf16[11,16,2,64,64]{4,3,2,1,0:T(8,128)(2,1)} %w2.1), custom_call_target="tpu_custom_call" | custom-call | tf_op jit(solution)/shard_map/pallas_call | solution.py:431
  136.4 2.4 %shard_map.38 = bf16[1024,1024]{1,0:T(8,128)(2,1)} custom-call(bf16[8,1024,128]{2,1,0:T(8,128)(2,1)} %bitcast.2), custom_call_target="tpu_custom_call" | custom-call | tf_op jit(solution)/shard_map/pallas_call | solution.py:453
